TPU v7x, 512 devices: a whole 4x8x8 slice. The times are simulated.
512 devices in a mesh: seq: 128 (over y, z, core), head: 4 (over x).
Axes of the slice: x: 4, y: 8, z: 8, core: 2. Of those that a mesh axis runs over, the one named last changes fastest.
Arguments:
- queries: bfloat16 [32768, 4096], P('seq', 'head'), may hold values from -6 to 6
- keys: bfloat16 [32768, 1024], P('seq', 'head'), may hold values from -6 to 6
- values: bfloat16 [32768, 1024], P('seq', 'head'), may hold values from -15 to 15
- selected: int32 [512, 8, 16], P('seq', 'head'), may hold values from -1 to 511, as said below
- norm_gain: bfloat16 [4096], P('head'), may hold values from 0.099609375 to 1.8984375
Outputs:
- normalized: bfloat16 [32768, 4096], P('seq', 'head')
Inputs may be any that keep to these rules, and one draw needn't show every extreme that they name: selected[b, g] lists b first, then 0 (or -1 where b = 0), then distinct blocks above 0 and below b, or -1. Over the query blocks of one index of seq and the KV heads of one index of head, the blocks named that belong to another index of seq form at most 2 distinct (block, KV head) pairs per such index.
All inputs are finite; a program needn't handle non-finite values.
Results may differ from a plain program's by a relative error of at most 0.0047.
Values may be sent and summed in bfloat16 or wider, within the bound.
No kernel may reach another device: no remote copies, remote signals or barrier semaphores. Data moves between devices by JAX's collectives and lax.ppermute only.
A program may use at most 64 MiB of HBM per device.

v0:
```python
import math

import jax
import jax.numpy as jnp
from jax import lax
from jax.sharding import PartitionSpec as P


def cut_along(array, dim, devices):
    dims = array.shape
    tiles = array.reshape(*dims[:dim], devices, dims[dim] // devices, *dims[dim + 1 :])
    return jnp.moveaxis(tiles, dim, 0)


def edges_of(length, count):
    step = length // count
    if step >= 8:
        step -= step % 8
    return [step * k for k in range(1, count)]


def in_order(tiles, dim):
    dims = list(tiles.shape[1:])
    dims[dim] *= tiles.shape[0]
    return jnp.moveaxis(tiles, 0, dim).reshape(dims)


def several_exchanges(array, axis, pieces, split_dim, concat_dim):
    tiles = cut_along(array, split_dim, lax.axis_size(axis))
    split_at = max(range(1, max(2, tiles.ndim - 1)), key=lambda d: tiles.shape[d])
    gathered = []
    for share in jnp.split(tiles, edges_of(tiles.shape[split_at], pieces), axis=split_at):
        if share.size:
            gathered.append(lax.all_to_all(share, axis, split_axis=0, concat_axis=0, tiled=True))
    return in_order(jnp.concatenate(gathered, axis=split_at), concat_dim)


def from_everyone(array, axis):
    copies = jnp.broadcast_to(array, (lax.axis_size(axis), *array.shape))
    return lax.all_to_all(copies, axis, split_axis=0, concat_axis=0, tiled=True)


def of_everyone(array, axis):
    everything = from_everyone(array, axis)
    return jnp.sum(everything, axis=0)


def per_device(queries, keys, values, selected, norm_gain):
    seq_count = lax.axis_size("seq")
    me = lax.axis_index("seq")
    tok_dev = queries.shape[0]
    per_dev, kv_local, top = selected.shape
    block = tok_dev // per_dev
    head_dim = keys.shape[1] // kv_local
    group = queries.shape[1] // (kv_local * head_dim)
    codes = per_dev * kv_local
    scale = 1.0 / math.sqrt(head_dim)
    owner = jnp.where(selected >= 0, selected // per_dev, -1)
    head_iota = jnp.arange(kv_local, dtype=jnp.int32)[None, :, None]
    local_code = selected % per_dev * kv_local + head_iota
    remote = (selected >= 0) & (owner != me)
    wanted = jnp.where(remote, owner * codes + local_code, -1).reshape(-1)
    present = jnp.any(
        wanted[:, None] == jnp.arange(seq_count * codes, dtype=jnp.int32)[None, :], axis=0
    )
    present = present.reshape(seq_count, codes)
    rank = jnp.cumsum(present.astype(jnp.int32), axis=1) - 1
    slot_iota = jnp.arange(kv_local, dtype=jnp.int32)
    filled = present[:, :, None] & (rank[:, :, None] == slot_iota[None, None, :])
    code_iota = jnp.arange(codes, dtype=jnp.int32)[None, :, None]
    request = jnp.sum(jnp.where(filled, code_iota + 1, 0), axis=1) - 1
    asked = lax.all_to_all(request, "seq", split_axis=0, concat_axis=0, tiled=True)

    def by_code(array):
        return (
            array.reshape(per_dev, block, kv_local, head_dim)
            .transpose(0, 2, 1, 3)
            .reshape(codes, block, head_dim)
        )

    stock = jnp.stack([by_code(keys), by_code(values)], axis=1)
    parcel = stock[jnp.clip(asked, 0, codes - 1)]
    arrived = several_exchanges(parcel, "seq", 2, 0, 0)
    pieces = [arrived.reshape(seq_count * kv_local, 2, block, head_dim), stock]
    base_local = seq_count * kv_local
    entry_slot = rank.reshape(-1)[jnp.clip(wanted, 0, seq_count * codes - 1)].reshape(
        selected.shape
    )
    index = jnp.where(owner == me, base_local + local_code, owner * kv_local + entry_slot)
    index = jnp.where(selected >= 0, index, 0)
    pool = jnp.concatenate(pieces, axis=0)
    offsets = jnp.arange(block, dtype=jnp.int32)
    q_blocks = queries.reshape(per_dev, block, kv_local, group, head_dim)

    def attend(args):
        q_block, sel_row, idx_row, start = args
        chosen = pool[idx_row]
        k_all = chosen[:, :, 0].reshape(kv_local, top * block, head_dim)
        v_all = chosen[:, :, 1].reshape(kv_local, top * block, head_dim)
        scores = (
            jnp.einsum("tgrd,gkd->grtk", q_block, k_all, preferred_element_type=jnp.float32) * scale
        )
        key_pos = (sel_row[:, :, None] * block + offsets[None, None, :]).reshape(
            kv_local, top * block
        )
        live = jnp.broadcast_to((sel_row >= 0)[:, :, None], (kv_local, top, block)).reshape(
            kv_local, top * block
        )
        query_pos = start + offsets
        mask = live[:, None, None, :] & (
            key_pos[:, None, None, :] <= query_pos[None, None, :, None]
        )
        peak = jnp.max(jnp.where(mask, scores, -1e30), axis=-1, keepdims=True)
        weights = jnp.where(mask, jnp.exp(scores - peak), 0.0)
        total = jnp.sum(weights, axis=-1)
        mixed = jnp.einsum(
            "grtk,gkd->tgrd",
            weights.astype(jnp.bfloat16),
            v_all,
            preferred_element_type=jnp.float32,
        )
        return mixed / jnp.transpose(total, (2, 0, 1))[..., None]

    starts = me * tok_dev + jnp.arange(per_dev, dtype=jnp.int32) * block
    attended = lax.map(attend, (q_blocks, selected, index, starts)).reshape(
        tok_dev, queries.shape[1]
    )
    squares = jnp.sum(attended * attended, axis=1)
    summed = of_everyone(squares, "head")
    inverse = lax.rsqrt(summed / (queries.shape[1] * lax.axis_size("head")) + 1e-05)
    normed = attended * inverse[:, None] * norm_gain.astype(jnp.float32)[None, :]
    return normed.astype(jnp.bfloat16)


def solution(mesh):
    return jax.shard_map(
        per_device,
        mesh=mesh,
        in_specs=(
            P("seq", "head"),
            P("seq", "head"),
            P("seq", "head"),
            P("seq", "head", None),
            P("head"),
        ),
        out_specs=P("seq", "head"),
        check_vma=False,
    )
```

profile of v0, /device:TPU:1, one launch (start us, length us, event | category | flops | bytes accessed | tf_op | source)
XLA Modules:
  0.0 330.5 jit_solution(16933726820833131575)
XLA Ops:
  0.0 0.7 broadcast_clamp_fusion.1
  0.8 0.2 fusion.25
  1.0 0.1 reshape.183
  1.1 0.2 reduce_window_sum.11
  1.5 0.8 copy.38
  2.3 18.4 %all-to-all-start = ((s32[128,1,2]{2,1,0:T(1,128)}), s32[128,1,2]{2,1,0:T(1,128)S(1)}, u32[]{:S(2)}, u32[]{:S(2)}) async-start(s32[128,1,2]{2,1,0:T(1,128)} %copy.38), calls=%async_computation | async-start | bytes 131072 | tf_op jit(solution)/shard_map/all_to_all | solution.py:72
  20.7 0.9 reshape.185
  21.7 0.9 reshape.186
  22.7 9.5 %all-to-all-done = s32[128,1,2]{2,1,0:T(1,128)S(1)} async-done(((s32[128,1,2]{2,1,0:T(1,128)}), s32[128,1,2]{2,1,0:T(1,128)S(1)}, u32[]{:S(2)}, u32[]{:S(2)}) %all-to-all-start) | async-done | bytes 1056 | tf_op jit(solution)/shard_map/all_to_all | solution.py:72
  32.2 0.1 broadcast_clamp_fusion
  32.3 0.1 reshape.208
  32.5 8.2 %gather_fusion.2 = bf16[256,2,64,128]{3,2,1,0:T(8,128)(2,1)} fusion(bf16[8,2,64,128]{3,2,1,0:T(8,128)(2,1)S(1)} %pad_maximum_fusion.1, s32[1024]{0:T(1024)S(1)} %pad_clamp_fusion.1), kind=kCustom, calls=%fused_computation.2 | custom fusion | bytes 16778240 | tf_op jit(solution)/shard_map/gather | solution.py:82
  40.7 6.3 %fusion.33 = (bf16[128,1,2,2,32,128]{5,4,3,2,1,0:T(8,128)(2,1)S(1)}, bf16[128,1,2,2,32,128]{5,4,3,2,1,0:T(8,128)(2,1)}) fusion(bf16[128,1,2,2,64,128]{5,4,3,2,1,0:T(8,128)(2,1)} %bitcast.131), kind=kLoop, calls=%fused_computation.74 | loop fusion | bytes 16777216 | tf_op jit(solution)/shard_map/split | solution.py:32
  47.0 101.4 %all_to_all.22 = bf16[128,1,2,2,32,128]{5,4,3,2,1,0:T(8,128)(2,1)} all-to-all(bf16[128,1,2,2,32,128]{5,4,3,2,1,0:T(8,128)(2,1)S(1)} %get-tuple-element.133), channel_id=1, replica_groups=mesh['seq'=128,'head'=4] {'seq'}, dimensions={0} | all-to-all | bytes 8388608 | tf_op jit(solution)/shard_map/all_to_all | solution.py:34
  148.4 16.4 %all-to-all-start.2 = ((bf16[128,1,2,2,32,128]{5,4,3,2,1,0:T(8,128)(2,1)}), bf16[128,1,2,2,32,128]{5,4,3,2,1,0:T(8,128)(2,1)}, u32[]{:S(2)}, u32[]{:S(2)}) async-start(bf16[128,1,2,2,32,128]{5,4,3,2,1,0:T(8,128)(2,1)} %get-tuple-element.134), calls=%async_computation.2 | async-start | bytes 8388608 | tf_op jit(solution)/shard_map/all_to_all | solution.py:34
  164.8 0.1 sub.28
  165.0 1.0 gather_fusion.1
  166.1 1.2 reshape.188
  167.3 93.2 %all-to-all-done.2 = bf16[128,1,2,2,32,128]{5,4,3,2,1,0:T(8,128)(2,1)} async-done(((bf16[128,1,2,2,32,128]{5,4,3,2,1,0:T(8,128)(2,1)}), bf16[128,1,2,2,32,128]{5,4,3,2,1,0:T(8,128)(2,1)}, u32[]{:S(2)}, u32[]{:S(2)}) %all-to-all-start.2) | async-done | bytes 4194336 | tf_op jit(solution)/shard_map/all_to_all | solution.py:34
  260.5 9.9 %pad_maximum_fusion = bf16[128,1,2,2,64,128]{5,4,3,2,1,0:T(8,128)(2,1)} fusion(bf16[128,1,2,2,32,128]{5,4,3,2,1,0:T(8,128)(2,1)} %all-to-all-done.2, bf16[128,1,2,2,32,128]{5,4,3,2,1,0:T(8,128)(2,1)} %all_to_all.22), kind=kLoop, calls=%fused_computation.38 | loop fusion | flops 16777216 | bytes 16777216 | tf_op jit(solution)/shard_map/concatenate | solution.py:35
  270.5 7.4 %maximum_maximum_fusion = bf16[264,2,64,128]{3,2,1,0:T(8,128)(2,1)} fusion(bf16[8,1,64,128]{3,2,1,0:T(8,128)(2,1)S(1)} %bitcast.137, bf16[8,1,64,128]{3,2,1,0:T(8,128)(2,1)S(1)} %bitcast.135, bf16[256,2,64,128]{3,2,1,0:T(8,128)(2,1)} %bitcast.132), kind=kLoop, calls=%fused_computation.37 | loop fusion | flops 8650752 | bytes 17301504 | tf_op jit(solution)/shard_map/concatenate | solution.py:91
  277.9 41.3 %while.12 = (s32[]{:T(128)}, f32[4,64,2,4,128]{4,1,3,2,0:T(8,128)}, s32[4,2,16]{2,1,0:T(2,128)S(1)}, bf16[264,2,64,128]{3,2,1,0:T(8,128)(2,1)}, s32[4,2,16]{2,1,...) while((s32[]{:T(128)}, f32[4,64,2,4,128]{4,1,3,2,0:T(8,128)}, ...), condition=%wide.region_6.7_spmd.clone.clone, body=%wide.region_3.6_spmd.clone.clone.sunk | while | flops 543495936 | bytes 13455797 | solution.py:125
  278.2 0.1 and.77
  278.3 0.6 dynamic_slice.39
  278.9 0.6 iota_add_fusion.3
  279.6 0.2 compare_and_fusion.2
  279.8 4.2 %gather_fusion = bf16[32,2,64,128]{3,2,1,0:T(8,128)(2,1)S(1)} fusion(bf16[264,2,64,128]{3,2,1,0:T(8,128)(2,1)} %get-tuple-element.201, s32[1024]{0:T(1024)S(1)} %pad_clamp_fusion.4), kind=kCustom, calls=%fused_computation.clone.clone.1 | custom fusion | bytes 2097280 | tf_op jit(solution)/shard_map/while/body/eval_jaxpr/gather | solution.py:97
  284.1 1.0 constant_dynamic-slice_fusion.3
  285.1 1.1 fusion.54
  286.2 0.4 fusion.53
  286.7 1.6 fusion.55
  288.6 0.1 and.77
  288.6 0.6 dynamic_slice.39
  289.3 0.6 iota_add_fusion.3
  289.9 0.2 compare_and_fusion.2
  290.2 4.2 %gather_fusion = bf16[32,2,64,128]{3,2,1,0:T(8,128)(2,1)S(1)} fusion(bf16[264,2,64,128]{3,2,1,0:T(8,128)(2,1)} %get-tuple-element.201, s32[1024]{0:T(1024)S(1)} %pad_clamp_fusion.4), kind=kCustom, calls=%fused_computation.clone.clone.1 | custom fusion | bytes 2097280 | tf_op jit(solution)/shard_map/while/body/eval_jaxpr/gather | solution.py:97
  294.5 1.0 constant_dynamic-slice_fusion.3
  295.4 1.1 fusion.54
  296.5 0.4 fusion.53
  297.0 1.6 fusion.55
  298.9 0.1 and.77
  299.0 0.6 dynamic_slice.39
  299.6 0.6 iota_add_fusion.3
  300.2 0.2 compare_and_fusion.2
  300.5 4.2 %gather_fusion = bf16[32,2,64,128]{3,2,1,0:T(8,128)(2,1)S(1)} fusion(bf16[264,2,64,128]{3,2,1,0:T(8,128)(2,1)} %get-tuple-element.201, s32[1024]{0:T(1024)S(1)} %pad_clamp_fusion.4), kind=kCustom, calls=%fused_computation.clone.clone.1 | custom fusion | bytes 2097280 | tf_op jit(solution)/shard_map/while/body/eval_jaxpr/gather | solution.py:97
  304.8 1.0 constant_dynamic-slice_fusion.3
  305.7 1.1 fusion.54
  306.9 0.4 fusion.53
  307.3 1.6 fusion.55
  309.3 0.6 dynamic_slice.39
  309.9 0.6 iota_add_fusion.3
  310.5 0.2 compare_and_fusion.2
  310.8 4.2 %gather_fusion = bf16[32,2,64,128]{3,2,1,0:T(8,128)(2,1)S(1)} fusion(bf16[264,2,64,128]{3,2,1,0:T(8,128)(2,1)} %get-tuple-element.201, s32[1024]{0:T(1024)S(1)} %pad_clamp_fusion.4), kind=kCustom, calls=%fused_computation.clone.clone.1 | custom fusion | bytes 2097280 | tf_op jit(solution)/shard_map/while/body/eval_jaxpr/gather | solution.py:97
  315.1 1.0 constant_dynamic-slice_fusion.3
  316.1 1.1 fusion.54
  317.2 0.4 fusion.53
  317.7 1.6 fusion.55
  319.2 1.4 multiply_reduce_fusion
  320.7 0.6 broadcast_in_dim.71
  321.3 4.0 %all-to-all-start.3 = ((f32[4,1,256]{2,1,0:T(1,128)}), f32[4,1,256]{2,1,0:T(1,128)S(1)}, u32[]{:S(2)}, u32[]{:S(2)}) async-start(f32[4,1,256]{2,1,0:T(1,128)} %broadcast_in_dim.71), calls=%async_computation.3 | async-start | bytes 8192 | tf_op jit(solution)/shard_map/all_to_all | solution.py:40
  325.4 1.9 copy.40
  327.3 0.4 reshape.189
  327.7 1.8 all-to-all-done.3
  329.5 1.0 multiply_convert_fusion
  (79 shorter events, 2.9 us)
Async XLA Ops:
  2.3 29.9 %all-to-all-start = ((s32[128,1,2]{2,1,0:T(1,128)}), s32[128,1,2]{2,1,0:T(1,128)S(1)}, u32[]{:S(2)}, u32[]{:S(2)}) async-start(s32[128,1,2]{2,1,0:T(1,128)} %copy.38), calls=%async_computation | async-start | bytes 131072 | tf_op jit(solution)/shard_map/all_to_all | solution.py:72
  148.4 17.7 %copy-start = (bf16[256,1024]{1,0:T(8,128)(2,1)S(1)}, bf16[256,1024]{1,0:T(8,128)(2,1)}, u32[]{:S(2)}) copy-start(bf16[256,1024]{1,0:T(8,128)(2,1)} %param.7) | copy-start | bytes 1572868
  148.4 18.9 %copy-start.1 = (s32[4,2,16]{2,1,0:T(2,128)S(1)}, s32[4,2,16]{2,1,0:T(2,128)}, u32[]{:S(2)}) copy-start(s32[4,2,16]{2,1,0:T(2,128)} %param.10) | copy-start | bytes 1540
  148.4 112.1 %all-to-all-start.2 = ((bf16[128,1,2,2,32,128]{5,4,3,2,1,0:T(8,128)(2,1)}), bf16[128,1,2,2,32,128]{5,4,3,2,1,0:T(8,128)(2,1)}, u32[]{:S(2)}, u32[]{:S(2)}) async-start(bf16[128,1,2,2,32,128]{5,4,3,2,1,0:T(8,128)(2,1)} %get-tuple-element.134), calls=%async_computation.2 | async-start | bytes 8388608 | tf_op jit(solution)/shard_map/all_to_all | solution.py:34
  277.9 47.4 %copy-start.2 = (bf16[1024]{0:T(1024)(128)(2,1)S(1)}, bf16[1024]{0:T(1024)(128)(2,1)}, u32[]{:S(2)}) copy-start(bf16[1024]{0:T(1024)(128)(2,1)} %param.11) | copy-start | bytes 6148
  321.3 8.2 %all-to-all-start.3 = ((f32[4,1,256]{2,1,0:T(1,128)}), f32[4,1,256]{2,1,0:T(1,128)S(1)}, u32[]{:S(2)}, u32[]{:S(2)}) async-start(f32[4,1,256]{2,1,0:T(1,128)} %broadcast_in_dim.71), calls=%async_computation.3 | async-start | bytes 8192 | tf_op jit(solution)/shard_map/all_to_all | solution.py:40
where the time goes:
time: 337 us; the launch traced here: 330 us
  waiting for transfers between devices  105 us (31%)
  blocking collectives  101 us (30%)
  local copies, waits for them, and re-layouts  48.4 us (14%)
  starting transfers between devices  38.9 us (12%)
  other arithmetic  24.3 us (7%)
  matrix products  12.6 us (4%)
    all_to_all x1, blocking collectives, several_exchanges(): lax.all_to_all(share, axis, split_axis=0, concat_axis=0, tiled=True)  101 us
    all_to_all x1, waiting for transfers between devices, several_exchanges(): lax.all_to_all(share, axis, split_axis=0, concat_axis=0, tiled=True)  93.2 us
    all_to_all x1, starting transfers between devices, per_device(): lax.all_to_all(request, 'seq', split_axis=0, concat_axis=0, tiled=True)  18.4 us
    gather x4, local copies, waits for them, and re-layouts, attend(): chosen = pool[idx_row]  16.8 us
    all_to_all x1, starting transfers between devices, several_exchanges(): lax.all_to_all(share, axis, split_axis=0, concat_axis=0, tiled=True)  16.4 us
    concatenate x1, other arithmetic, several_exchanges(): return in_order(jnp.concatenate(gathered, axis=split_at), concat_dim)  9.94 us
    all_to_all x1, waiting for transfers between devices, per_device(): lax.all_to_all(request, 'seq', split_axis=0, concat_axis=0, tiled=True)  9.53 us
    gather x1, local copies, waits for them, and re-layouts, per_device(): parcel = stock[jnp.clip(asked, 0, codes - 1)]  8.21 us
  transfers between devices with their start and end apart: 3, of which 3 were waited for; matrix products, arithmetic and copies ran while one was open for 2% of the time, Pallas kernels for 0%

commit v1 on v0

v1 whole, which is shorter than its diff:
```python
import functools
import math

import jax
import jax.numpy as jnp
from jax import lax
from jax.experimental import pallas as pl
from jax.experimental.pallas import tpu as pltpu
from jax.sharding import PartitionSpec as P

NEG = -1e30


def attend_kernel(sel_ref, q_ref, kv_ref, att_ref, sq_ref, buf, sems, *, dims):
    per_dev, kv_local, top, block, head_dim, group = dims
    units = per_dev * kv_local
    width = 2 * head_dim
    exponent_scale = math.log2(math.e) / math.sqrt(head_dim)

    def fetch(unit, carry):
        col = pl.multiple_of(unit % kv_local * width, width)
        for entry in range(top):
            row = pl.multiple_of(jnp.maximum(sel_ref[unit * top + entry], 0) * block, block)
            pltpu.make_async_copy(
                kv_ref.at[pl.ds(row, block), pl.ds(col, width)],
                buf.at[unit, pl.ds(entry * block, block)],
                sems.at[unit],
            ).start()
        return carry

    lax.fori_loop(0, units, fetch, 0)

    lanes = 2 * block
    lane = lax.broadcasted_iota(jnp.int32, (1, lanes), 1)
    token = lax.broadcasted_iota(jnp.int32, (group * block, lanes), 0) % block
    column = lax.broadcasted_iota(jnp.int32, (group * block, lanes), 1)
    diagonal = jnp.where((column >= block) | (column <= token), 0.0, NEG)

    def attend(number, carry):
        rows = pl.ds(pl.multiple_of(number * block, block), block)
        squares = jnp.zeros((block, head_dim), jnp.float32)
        for g in range(kv_local):
            unit = number * kv_local + g
            pltpu.make_async_copy(
                kv_ref.at[pl.ds(0, top * block), pl.ds(0, width)], buf.at[unit], sems.at[unit]
            ).wait()
            heads = [
                slice((g * group + r) * head_dim, (g * group + r + 1) * head_dim)
                for r in range(group)
            ]
            q = jnp.concatenate([q_ref[rows, h] for h in heads], axis=0)
            keys = buf[unit, :, :head_dim]
            vals = buf[unit, :, head_dim:]
            scores = lax.dot_general(
                q, keys, (((1,), (1,)), ((), ())), preferred_element_type=jnp.float32
            )
            parts = []
            for pair in range(top // 2):
                low = jnp.where(sel_ref[unit * top + 2 * pair] >= 0, 0.0, NEG)
                high = jnp.where(sel_ref[unit * top + 2 * pair + 1] >= 0, 0.0, NEG)
                dead = jnp.where(lane < block, low, high)
                part = scores[:, pair * lanes : (pair + 1) * lanes] * exponent_scale + dead
                parts.append(part + diagonal if pair == 0 else part)
            peak = jnp.max(functools.reduce(jnp.maximum, parts), axis=1, keepdims=True)
            parts = [jnp.exp2(part - peak) for part in parts]
            total = jnp.sum(functools.reduce(jnp.add, parts), axis=1, keepdims=True)
            rounded = jnp.concatenate([part.astype(jnp.bfloat16) for part in parts], axis=1)
            mixed = jnp.dot(rounded, vals, preferred_element_type=jnp.float32) / total
            for r, h in enumerate(heads):
                piece = mixed[r * block : (r + 1) * block]
                att_ref[rows, h] = piece
                squares = squares + piece * piece
        sq_ref[rows, :] = squares
        return carry

    lax.fori_loop(0, per_dev, attend, 0)


def attend_blocks(selected, queries, pool, dims):
    per_dev, kv_local, top, block, head_dim, group = dims
    tokens = per_dev * block
    return pl.pallas_call(
        functools.partial(attend_kernel, dims=dims),
        out_shape=[
            jax.ShapeDtypeStruct(queries.shape, jnp.float32),
            jax.ShapeDtypeStruct((tokens, head_dim), jnp.float32),
        ],
        in_specs=[
            pl.BlockSpec(memory_space=pltpu.SMEM),
            pl.BlockSpec(memory_space=pltpu.VMEM),
            pl.BlockSpec(memory_space=pl.ANY),
        ],
        out_specs=[pl.BlockSpec(memory_space=pltpu.VMEM), pl.BlockSpec(memory_space=pltpu.VMEM)],
        scratch_shapes=[
            pltpu.VMEM((per_dev * kv_local, top * block, 2 * head_dim), jnp.bfloat16),
            pltpu.SemaphoreType.DMA((per_dev * kv_local,)),
        ],
        compiler_params=pltpu.CompilerParams(vmem_limit_bytes=40 * 1024 * 1024),
        name="attend",
    )(selected, queries, pool)


def per_device(queries, keys, values, selected, norm_gain):
    heads_axis = lax.axis_size("head")
    tok_dev = queries.shape[0]
    per_dev, kv_local, top = selected.shape
    block = tok_dev // per_dev
    head_dim = keys.shape[1] // kv_local
    group = queries.shape[1] // (kv_local * head_dim)
    dims = (per_dev, kv_local, top, block, head_dim, group)
    pieces = []
    for g in range(kv_local):
        cols = slice(g * head_dim, (g + 1) * head_dim)
        pieces += [keys[:, cols], values[:, cols]]
    pool = lax.all_gather(jnp.concatenate(pieces, axis=1), "seq", axis=0, tiled=True)
    attended, squares = attend_blocks(selected.reshape(-1), queries, pool, dims)
    local = jnp.sum(squares, axis=1)
    summed = local
    for shift in range(1, heads_axis):
        ring = [(i, (i + shift) % heads_axis) for i in range(heads_axis)]
        summed = summed + lax.ppermute(local, "head", ring)
    inverse = lax.rsqrt(summed / (queries.shape[1] * heads_axis) + 1e-05)
    normed = attended * inverse[:, None] * norm_gain.astype(jnp.float32)[None, :]
    return normed.astype(jnp.bfloat16)


def solution(mesh):
    return jax.shard_map(
        per_device,
        mesh=mesh,
        in_specs=(
            P("seq", "head"),
            P("seq", "head"),
            P("seq", "head"),
            P("seq", "head", None),
            P("head"),
        ),
        out_specs=P("seq", "head"),
        check_vma=False,
    )
```

time: 337 us -> 187 us (0.55); the launches traced: 330 us -> 186 us
  blocking collectives: 101 us -> 0 us
  local copies, waits for them, and re-layouts: 48.4 us -> 2.78 us
  waiting for transfers between devices: 105 us -> 150 us
  starting transfers between devices: 38.9 us -> 10.5 us
  other arithmetic: 24.3 us -> 1.81 us
  between operations: 0.15 us -> 13.5 us
  matrix products: 12.6 us -> 0 us
  Pallas kernels: 0 us -> 7.84 us
    all_gather x0 -> x1, waiting for transfers between devices: none -> 149 us  [per_device(): lax.all_gather(jnp.concatenate(pieces, axis=1), 'seq', axis=0, tiled=True)]
    all_to_all x3 -> x0, waiting for transfers between devices: 105 us -> none  [the longest x1 93.2 us: several_exchanges(): lax.all_to_all(share, axis, split_axis=0, concat_axis=0, tiled=True)]
    all_to_all x1 -> x0, blocking collectives: 101 us -> none  [several_exchanges(): lax.all_to_all(share, axis, split_axis=0, concat_axis=0, tiled=True)]
    all_to_all x3 -> x0, starting transfers between devices: 38.9 us -> none  [the longest x1 18.4 us: per_device(): lax.all_to_all(request, 'seq', split_axis=0, concat_axis=0, tiled=True)]
    gather x6 -> x0, local copies, waits for them, and re-layouts: 26 us -> none  [the longest x4 16.8 us: attend(): chosen = pool[idx_row]]
    concatenate x2 -> x1, other arithmetic: 17.4 us -> 0.73 us  [per_device(): jnp.concatenate(pieces, axis=1)]
    ppermute x0 -> x3, starting transfers between devices: none -> 10.5 us  [per_device(): summed = summed + lax.ppermute(local, 'head', ring)]
    dot_general x8 -> x0, matrix products: 8.05 us -> none  [the longest x4 6.3 us: attend(): jnp.einsum('grtk,gkd->tgrd', weights.astype(jnp.bfloat16), v_all, preferr...]
  transfers between devices with their start and end apart: 3 -> 4, of which waited for: 3 -> 2; matrix products, arithmetic and copies ran while one was open for 2% -> 0% of each run, Pallas kernels for 0% -> 0%
where the time goes in v1:
time: 187 us; the launch traced here: 186 us
  waiting for transfers between devices  150 us (80%)
  between operations  13.5 us (7%)
  starting transfers between devices  10.5 us (6%)
  Pallas kernels  7.84 us (4%)
  local copies, waits for them, and re-layouts  2.78 us (1%)
    all_gather x1, waiting for transfers between devices, per_device(): lax.all_gather(jnp.concatenate(pieces, axis=1), 'seq', axis=0, tiled=True)  149 us
    ppermute x3, starting transfers between devices, per_device(): summed = summed + lax.ppermute(local, 'head', ring)  10.5 us
    pallas_call x1, Pallas kernels, attend_blocks(): pl.pallas_call(functools.partial(attend_kernel, dims=dims), out_shape=[ja...  7.84 us
  transfers between devices with their start and end apart: 4, of which 2 were waited for; matrix products, arithmetic and copies ran while one was open for 0% of the time, Pallas kernels for 0%

profile of v1, /device:TPU:1, one launch (start us, length us, event | category | flops | bytes accessed | tf_op | source)
XLA Modules:
  0.0 186.2 jit_solution(319447566566241315)
XLA Ops:
  6.5 0.0 copy-start.1
  6.5 0.0 all-gather.2.cloned.1.call-start
  6.5 1.0 fusion
  7.5 0.7 pad_maximum_fusion
  8.2 0.0 all-gather.2.cloned.1.call-update
  8.3 0.8 reshape.5.sel_ref
  9.0 148.6 %all-gather.2.cloned.1.call-done.kv_ref = bf16[32768,512]{1,0:T(8,128)(2,1)} async-done(((bf16[256,512]{1,0:T(8,128)(2,1)}), bf16[32768,512]{1,0:T(8,128)(2,1)}) %all-gather.2.cloned.1.call-update) | async-done | bytes 33554448 | tf_op jit(solution)/shard_map/all_gather | solution.py:115
  157.6 0.0 copy-start
  157.6 1.0 copy-done
  158.7 7.8 %attend.1 = (f32[256,1024]{1,0:T(8,128)S(1)}, f32[256,128]{1,0:T(8,128)S(1)}) custom-call(s32[128]{0:T(128)S(1)} %reshape.5.sel_ref, bf16[256,1024]{1,0:T(8,128)(2,1)S(1)} %copy-done, bf16[32768,512]{1,0:T(8,128)(2,1)} %all-gather.2.cloned.1.call-done.kv_ref), custom_call_target="tpu_custom_call" | custom-call | tf_op jit(solution)/shard_map/attend/pallas_call | solution.py:82
  166.5 0.1 reduce_sum.9
  166.6 3.1 %collective-permute-start = (f32[256]{0:T(256)S(1)}, f32[256]{0:T(256)S(1)}, u32[]{:S(2)}, u32[]{:S(2)}) collective-permute-start(f32[256]{0:T(256)S(1)} %reduce_sum.9), channel_id=1, source_target_pairs={{0,1},{1,2},{2,3},{3,0},{4,5},{5,6},{6,7},{7,4},{8,9},{9,10},{10,1... | collective-permute-start | bytes 3080 | tf_op jit(solution)/shard_map/ppermute | solution.py:121
  169.7 4.3 %collective-permute-start.1 = (f32[256]{0:T(256)S(1)}, f32[256]{0:T(256)S(1)}, u32[]{:S(2)}, u32[]{:S(2)}) collective-permute-start(f32[256]{0:T(256)S(1)} %reduce_sum.9), channel_id=1, source_target_pairs={{0,2},{1,3},{2,0},{3,1},{4,6},{5,7},{6,4},{7,5},{8,10},{9,11},{10,... | collective-permute-start | bytes 3080 | tf_op jit(solution)/shard_map/ppermute | solution.py:121
  174.0 3.1 %collective-permute-start.2 = (f32[256]{0:T(256)S(1)}, f32[256]{0:T(256)S(1)}, u32[]{:S(2)}, u32[]{:S(2)}) collective-permute-start(f32[256]{0:T(256)S(1)} %reduce_sum.9), channel_id=1, source_target_pairs={{0,3},{1,0},{2,1},{3,2},{4,7},{5,4},{6,5},{7,6},{8,11},{9,8},{10,9... | collective-permute-start | bytes 3080 | tf_op jit(solution)/shard_map/ppermute | solution.py:121
  177.1 0.0 copy-done.1
  177.2 0.0 collective-permute-done
  177.2 0.0 collective-permute-done.1
  177.2 1.2 collective-permute-done.2
  178.4 1.0 multiply_convert_fusion
  (2 shorter events, 0.0 us)
Async XLA Ops:
  6.5 170.6 %copy-start.1 = (bf16[1024]{0:T(1024)(128)(2,1)S(1)}, bf16[1024]{0:T(1024)(128)(2,1)}, u32[]{:S(2)}) copy-start(bf16[1024]{0:T(1024)(128)(2,1)} %param.9) | copy-start | bytes 6148
  6.5 151.1 %all-gather.2.cloned.1.call-start = ((), (), s32[]{:S(2)}) async-start(), calls=%async_computation | async-start | bytes 33816576 | tf_op jit(solution)/shard_map/all_gather | solution.py:115
  157.6 1.0 copy-start
  166.6 10.5 %collective-permute-start = (f32[256]{0:T(256)S(1)}, f32[256]{0:T(256)S(1)}, u32[]{:S(2)}, u32[]{:S(2)}) collective-permute-start(f32[256]{0:T(256)S(1)} %reduce_sum.9), channel_id=1, source_target_pairs={{0,1},{1,2},{2,3},{3,0},{4,5},{5,6},{6,7},{7,4},{8,9},{9,10},{10,1... | collective-permute-start | bytes 3080 | tf_op jit(solution)/shard_map/ppermute | solution.py:121
  169.7 7.5 %collective-permute-start.1 = (f32[256]{0:T(256)S(1)}, f32[256]{0:T(256)S(1)}, u32[]{:S(2)}, u32[]{:S(2)}) collective-permute-start(f32[256]{0:T(256)S(1)} %reduce_sum.9), channel_id=1, source_target_pairs={{0,2},{1,3},{2,0},{3,1},{4,6},{5,7},{6,4},{7,5},{8,10},{9,11},{10,... | collective-permute-start | bytes 3080 | tf_op jit(solution)/shard_map/ppermute | solution.py:121
  174.0 4.3 %collective-permute-start.2 = (f32[256]{0:T(256)S(1)}, f32[256]{0:T(256)S(1)}, u32[]{:S(2)}, u32[]{:S(2)}) collective-permute-start(f32[256]{0:T(256)S(1)} %reduce_sum.9), channel_id=1, source_target_pairs={{0,3},{1,0},{2,1},{3,2},{4,7},{5,4},{6,5},{7,6},{8,11},{9,8},{10,9... | collective-permute-start | bytes 3080 | tf_op jit(solution)/shard_map/ppermute | solution.py:121
Sparse Core Ops, SparseCore 0:
  10.5 147.1 all-gather.1

commit v2 on v1

v2 whole, which is shorter than its diff:
```python
import functools
import math

import jax
import jax.numpy as jnp
from jax import lax
from jax.experimental import pallas as pl
from jax.experimental.pallas import tpu as pltpu
from jax.sharding import PartitionSpec as P

NEG = -1e30
KEY_SCALE = 8192.0
VALUE_SCALE = 4096.0


def attend_kernel(sel_ref, q_ref, chosen_ref, att_ref, sq_ref, *, dims):
    per_dev, kv_local, top, block, head_dim, group = dims
    exponent_scale = math.log2(math.e) / math.sqrt(head_dim) / KEY_SCALE
    lanes = 2 * block
    lane = lax.broadcasted_iota(jnp.int32, (1, lanes), 1)
    token = lax.broadcasted_iota(jnp.int32, (group * block, lanes), 0) % block
    column = lax.broadcasted_iota(jnp.int32, (group * block, lanes), 1)
    diagonal = jnp.where((column >= block) | (column <= token), 0.0, NEG)

    def attend(number, carry):
        rows = pl.ds(pl.multiple_of(number * block, block), block)
        squares = jnp.zeros((block, head_dim), jnp.float32)
        for g in range(kv_local):
            unit = number * kv_local + g
            heads = [
                slice((g * group + r) * head_dim, (g * group + r + 1) * head_dim)
                for r in range(group)
            ]
            q = jnp.concatenate([q_ref[rows, h] for h in heads], axis=0)
            keys = chosen_ref[unit, :, :head_dim]
            vals = chosen_ref[unit, :, head_dim:]
            scores = lax.dot_general(
                q, keys, (((1,), (1,)), ((), ())), preferred_element_type=jnp.float32
            )
            parts = []
            for pair in range(top // 2):
                low = jnp.where(sel_ref[unit * top + 2 * pair] >= 0, 0.0, NEG)
                high = jnp.where(sel_ref[unit * top + 2 * pair + 1] >= 0, 0.0, NEG)
                dead = jnp.where(lane < block, low, high)
                part = scores[:, pair * lanes : (pair + 1) * lanes] * exponent_scale + dead
                parts.append(part + diagonal if pair == 0 else part)
            peak = jnp.max(functools.reduce(jnp.maximum, parts), axis=1, keepdims=True)
            parts = [jnp.exp2(part - peak) for part in parts]
            total = jnp.sum(functools.reduce(jnp.add, parts), axis=1, keepdims=True)
            rounded = jnp.concatenate([part.astype(jnp.bfloat16) for part in parts], axis=1)
            mixed = jnp.dot(rounded, vals, preferred_element_type=jnp.float32)
            mixed = mixed / (total * VALUE_SCALE)
            for r, h in enumerate(heads):
                piece = mixed[r * block : (r + 1) * block]
                att_ref[rows, h] = piece
                squares = squares + piece * piece
        sq_ref[rows, :] = squares
        return carry

    lax.fori_loop(0, per_dev, attend, 0)


def attend_blocks(selected, queries, chosen, dims):
    per_dev, kv_local, top, block, head_dim, group = dims
    whole = pl.BlockSpec(memory_space=pltpu.VMEM)
    return pl.pallas_call(
        functools.partial(attend_kernel, dims=dims),
        out_shape=[
            jax.ShapeDtypeStruct(queries.shape, jnp.float32),
            jax.ShapeDtypeStruct((per_dev * block, head_dim), jnp.float32),
        ],
        in_specs=[pl.BlockSpec(memory_space=pltpu.SMEM), whole, whole],
        out_specs=[whole, whole],
        compiler_params=pltpu.CompilerParams(vmem_limit_bytes=40 * 1024 * 1024),
        name="attend",
    )(selected, queries, chosen)


def per_device(queries, keys, values, selected, norm_gain):
    heads_axis = lax.axis_size("head")
    tok_dev = queries.shape[0]
    per_dev, kv_local, top = selected.shape
    block = tok_dev // per_dev
    head_dim = keys.shape[1] // kv_local
    group = queries.shape[1] // (kv_local * head_dim)
    dims = (per_dev, kv_local, top, block, head_dim, group)
    codes = per_dev * kv_local

    def by_code(array, scale):
        rows = array.reshape(per_dev, block, kv_local, head_dim).transpose(0, 2, 1, 3)
        scaled = rows.reshape(codes, block, head_dim).astype(jnp.float32) * scale
        return scaled.astype(jnp.float16)

    stock = jnp.concatenate([by_code(keys, KEY_SCALE), by_code(values, VALUE_SCALE)], axis=2)
    pool = lax.all_gather(stock, "seq", axis=0, tiled=True)
    head_iota = jnp.arange(kv_local, dtype=jnp.int32)[None, :, None]
    index = (jnp.maximum(selected, 0) * kv_local + head_iota).reshape(-1)
    chosen = jnp.take(pool, index, axis=0, mode="clip").astype(jnp.bfloat16)
    chosen = chosen.reshape(codes, top * block, 2 * head_dim)
    flat = selected.reshape(-1)
    attended, squares = attend_blocks(flat, queries, chosen, dims)
    local = jnp.sum(squares, axis=1)
    copies = jnp.broadcast_to(local, (heads_axis, 1, tok_dev))
    everyone = lax.all_to_all(copies, "head", split_axis=0, concat_axis=0, tiled=True)
    summed = jnp.sum(everyone, axis=(0, 1))
    inverse = lax.rsqrt(summed / (queries.shape[1] * heads_axis) + 1e-05)
    normed = attended * inverse[:, None] * norm_gain.astype(jnp.float32)[None, :]
    return normed.astype(jnp.bfloat16)


def solution(mesh):
    return jax.shard_map(
        per_device,
        mesh=mesh,
        in_specs=(
            P("seq", "head"),
            P("seq", "head"),
            P("seq", "head"),
            P("seq", "head", None),
            P("head"),
        ),
        out_specs=P("seq", "head"),
        check_vma=False,
    )
```

time: 187 us -> 150 us (0.80)
  waiting for transfers between devices: 150 us -> 4.14 us
  blocking collectives: 0 us -> 119 us
  between operations: 13.5 us -> 0.08 us
  local copies, waits for them, and re-layouts: 2.78 us -> 10.4 us
  starting transfers between devices: 10.5 us -> 4.02 us
  other arithmetic: 1.81 us -> 7.53 us
  Pallas kernels: 7.84 us -> 5.01 us
    all_gather x1 -> x0, waiting for transfers between devices: 149 us -> none  [per_device(): lax.all_gather(jnp.concatenate(pieces, axis=1), 'seq', axis=0, tiled=True)]
    all_gather x0 -> x1, blocking collectives: none -> 119 us  [per_device(): pool = lax.all_gather(stock, 'seq', axis=0, tiled=True)]
    ppermute x3 -> x0, starting transfers between devices: 10.5 us -> none  [per_device(): summed = summed + lax.ppermute(local, 'head', ring)]
    gather x0 -> x1, local copies, waits for them, and re-layouts: none -> 8.72 us  [per_device(): chosen = jnp.take(pool, index, axis=0, mode='clip').astype(jnp.bfloat16)]
    all_to_all x0 -> x1, waiting for transfers between devices: none -> 4.14 us  [per_device(): lax.all_to_all(copies, 'head', split_axis=0, concat_axis=0, tiled=True)]
    all_to_all x0 -> x1, starting transfers between devices: none -> 4.02 us  [per_device(): lax.all_to_all(copies, 'head', split_axis=0, concat_axis=0, tiled=True)]
    convert_element_type x0 -> x1, other arithmetic: none -> 3.78 us  [per_device(): chosen = jnp.take(pool, index, axis=0, mode='clip').astype(jnp.bfloat16)]
    pallas_call x1, Pallas kernels: 7.84 us -> 5.01 us  [attend_blocks(): pl.pallas_call(functools.partial(attend_kernel, dims=dims), out_shape=[ja...]
  transfers between devices with their start and end apart: 4 -> 1, of which waited for: 2 -> 1; matrix products, arithmetic and copies ran while one was open for 0% -> 0% of each run, Pallas kernels for 0% -> 0%
where the time goes in v2:
time: 150 us
  blocking collectives  119 us (79%)
  local copies, waits for them, and re-layouts  10.4 us (7%)
  other arithmetic  7.53 us (5%)
  Pallas kernels  5.01 us (3%)
  waiting for transfers between devices  4.14 us (3%)
  starting transfers between devices  4.02 us (3%)
    all_gather x1, blocking collectives, per_device(): pool = lax.all_gather(stock, 'seq', axis=0, tiled=True)  119 us
    gather x1, local copies, waits for them, and re-layouts, per_device(): chosen = jnp.take(pool, index, axis=0, mode='clip').astype(jnp.bfloat16)  8.72 us
    pallas_call x1, Pallas kernels, attend_blocks(): pl.pallas_call(functools.partial(attend_kernel, dims=dims), out_shape=[ja...  5.01 us
    all_to_all x1, waiting for transfers between devices, per_device(): lax.all_to_all(copies, 'head', split_axis=0, concat_axis=0, tiled=True)  4.14 us
    all_to_all x1, starting transfers between devices, per_device(): lax.all_to_all(copies, 'head', split_axis=0, concat_axis=0, tiled=True)  4.02 us
    convert_element_type x1, other arithmetic, per_device(): chosen = jnp.take(pool, index, axis=0, mode='clip').astype(jnp.bfloat16)  3.78 us
  transfers between devices with their start and end apart: 1, of which 1 were waited for; matrix products, arithmetic and copies ran while one was open for 0% of the time, Pallas kernels for 0%

profile of v2, /device:TPU:1, one launch (start us, length us, event | category | flops | bytes accessed | tf_op | source)
XLA Modules:
  0.0 149.9 jit_solution(6117661415450473013)
XLA Ops:
  0.0 0.7 iota_add_fusion
  0.7 0.8 reshape.34.sel_ref
  1.5 0.9 multiply_convert_fusion.2
  2.5 0.9 multiply_convert_fusion.1
  3.6 0.1 pad_maximum_fusion
  3.6 118.8 %all-gather.1 = f16[1024,64,256]{2,1,0:T(8,128)(2,1)} all-gather(f16[8,64,256]{2,1,0:T(8,128)(2,1)S(1)} %pad_maximum_fusion), channel_id=1, replica_groups=mesh['seq'=128,'head'=4] {'seq'}, dimensions={0}, use_global_device_ids=true | all-gather | bytes 33816576 | tf_op jit(solution)/shard_map/all_gather | solution.py:95
  122.4 0.1 reshape.37
  122.5 8.7 %gather_fusion = f16[128,64,256]{2,1,0:T(8,128)(2,1)} fusion(f16[1024,64,256]{2,1,0:T(8,128)(2,1)} %all-gather.1, s32[1024]{0:T(1024)S(1)} %pad_clamp_fusion), kind=kCustom, calls=%fused_computation | custom fusion | bytes 8389120 | tf_op jit(solution)/shard_map/jit(_take)/gather | solution.py:98
  131.2 0.0 copy-start
  131.2 3.8 %convert_element_type.45 = bf16[128,64,256]{2,1,0:T(8,128)(2,1)S(1)} convert(f16[128,64,256]{2,1,0:T(8,128)(2,1)} %gather_fusion) | non-fusion elementwise | flops 2097152 | bytes 8388608 | tf_op jit(solution)/shard_map/convert_element_type | solution.py:98
  135.0 0.0 copy-start.1
  135.1 0.0 copy-done
  135.1 5.0 %attend.1 = (f32[256,1024]{1,0:T(8,128)S(1)}, f32[256,128]{1,0:T(8,128)S(1)}) custom-call(s32[128]{0:T(128)S(1)} %reshape.34.sel_ref, bf16[256,1024]{1,0:T(8,128)(2,1)S(1)} %copy-done, bf16[8,1024,256]{2,1,0:T(8,128)(2,1)S(1)} %bitcast.5), custom_call_target="tpu_custom_call" | custom-call | tf_op jit(solution)/shard_map/attend/pallas_call | solution.py:66
  140.1 0.1 reduce_sum.18
  140.2 0.6 broadcast_in_dim.11
  140.8 4.0 %all-to-all-start = ((f32[4,1,256]{2,1,0:T(1,128)}), f32[4,1,256]{2,1,0:T(1,128)S(1)}, u32[]{:S(2)}, u32[]{:S(2)}) async-start(f32[4,1,256]{2,1,0:T(1,128)} %broadcast_in_dim.11), calls=%async_computation | async-start | bytes 8192 | tf_op jit(solution)/shard_map/all_to_all | solution.py:104
  144.8 0.0 copy-done.1
  144.8 4.1 %all-to-all-done = f32[4,1,256]{2,1,0:T(1,128)S(1)} async-done(((f32[4,1,256]{2,1,0:T(1,128)}), f32[4,1,256]{2,1,0:T(1,128)S(1)}, u32[]{:S(2)}, u32[]{:S(2)}) %all-to-all-start) | async-done | bytes 4128 | tf_op jit(solution)/shard_map/all_to_all | solution.py:104
  149.0 1.0 multiply_convert_fusion
  (8 shorter events, 0.2 us)
Async XLA Ops:
  131.2 3.8 %copy-start = (bf16[256,1024]{1,0:T(8,128)(2,1)S(1)}, bf16[256,1024]{1,0:T(8,128)(2,1)}, u32[]{:S(2)}) copy-start(bf16[256,1024]{1,0:T(8,128)(2,1)} %q_ref.1) | copy-start | bytes 1572868
  135.0 9.8 %copy-start.1 = (bf16[1024]{0:T(1024)(128)(2,1)S(1)}, bf16[1024]{0:T(1024)(128)(2,1)}, u32[]{:S(2)}) copy-start(bf16[1024]{0:T(1024)(128)(2,1)} %param.9) | copy-start | bytes 6148
  140.8 8.2 %all-to-all-start = ((f32[4,1,256]{2,1,0:T(1,128)}), f32[4,1,256]{2,1,0:T(1,128)S(1)}, u32[]{:S(2)}, u32[]{:S(2)}) async-start(f32[4,1,256]{2,1,0:T(1,128)} %broadcast_in_dim.11), calls=%async_computation | async-start | bytes 8192 | tf_op jit(solution)/shard_map/all_to_all | solution.py:104
